TPU v7x, 32 devices: a whole 2x2x4 slice. The times are simulated.
32 devices in a mesh: row: 4 (over x, core), col: 8 (over z, y).
Axes of the slice: x: 2, y: 2, z: 4, core: 2. Of those that a mesh axis runs over, the one named last changes fastest.
Arguments:
- tensor: float32 [1024, 32, 1024], P(None, 'row', 'col'), may hold values from -60 to 60, as said below
- factor_two: float32 [32, 32], P('row'), may hold values from -1 to 1
- factor_three: float32 [32, 32], P('col'), may hold values from -1 to 1
- factor_four: float32 [32, 16], replicated, may hold values from -1 to 1
- factor_init: float32 [1024, 64], replicated, may hold values from -6 to 6
Outputs:
- factor_new: float32 [1024, 64], replicated
- core: float32 [64, 32, 32, 16], P(None, 'row', 'col')
Inputs may be any that keep to these rules, and one draw needn't show every extreme that they name: `tensor`: scales vary from slab to slab.
All inputs are finite; a program needn't handle non-finite values.
Results may differ from a plain program's by a relative error of at most 0.00013.
Values sent between devices are 32-bit elements; how exact they have to be, the bound alone decides.
A program may use at most 128 MiB of HBM per device.

v0:
```python
import jax
import jax.numpy as jnp
from jax import lax
from jax.sharding import PartitionSpec as P


def shards(tensor, factor_two, factor_three, factor_four, factor_init):
    highest = lax.Precision.HIGHEST
    first_len = tensor.shape[0]
    local_two = tensor.shape[1]
    fourth_len = factor_four.shape[0]
    local_three = tensor.shape[2] // fourth_len
    rank_one = factor_init.shape[1]
    data = tensor.reshape(first_len, local_two, local_three, fourth_len)
    fourth = jnp.einsum("abcd,de->abce", data, factor_four, precision=highest)
    whole_two = lax.all_gather(factor_two, "row", axis=0, tiled=True)
    spread_two = lax.all_to_all(fourth, "row", split_axis=0, concat_axis=1, tiled=True)
    projected_two = jnp.einsum("abce,bg->agce", spread_two, whole_two, precision=highest)
    partial_two = lax.all_to_all(projected_two, "row", split_axis=1, concat_axis=0, tiled=True)
    whole_three = lax.all_gather(factor_three, "col", axis=0, tiled=True)
    spread_three = lax.all_to_all(partial_two, "col", split_axis=0, concat_axis=2, tiled=True)
    projected_three = jnp.einsum("agce,cf->agfe", spread_three, whole_three, precision=highest)
    block = lax.all_to_all(projected_three, "col", split_axis=2, concat_axis=0, tiled=True)
    columns = block.reshape(first_len, -1)
    basis = factor_init
    local_gram = jnp.dot(columns, columns.T, precision=highest, preferred_element_type=jnp.float32)
    gram = lax.psum(local_gram, ("row", "col"))
    image = jnp.dot(gram, basis, precision=highest, preferred_element_type=jnp.float32)
    square = jnp.dot(image.T, image, precision=highest, preferred_element_type=jnp.float32)
    lower = jnp.linalg.cholesky(square)
    basis = jax.scipy.linalg.solve_triangular(lower, image.T, lower=True).T
    core = jnp.dot(basis.T, columns, precision=highest, preferred_element_type=jnp.float32)
    return (basis, core.reshape(rank_one, block.shape[1], block.shape[2], block.shape[3]))


def solution(mesh):
    in_specs = (P(None, "row", "col"), P("row", None), P("col", None), P(), P())
    out_specs = (P(), P(None, "row", "col", None))
    return jax.shard_map(shards, mesh=mesh, in_specs=in_specs, out_specs=out_specs, check_vma=False)
```

profile of v0, /device:TPU:0, one launch (start us, length us, event | category | flops | bytes accessed | tf_op | source)
XLA Modules:
  0.0 512.5 jit_solution(1816454857235836736)
XLA Ops:
  7.2 0.0 copy-start
  7.2 0.0 copy-start.4
  7.2 5.5 %copy.18 = f32[1024,8,128]{0,2,1:T(8,128)} copy(f32[1024,8,128]{2,1,0:T(8,128)} %param.5) | data formatting | bytes 8388608 | tf_op args[0]
  12.6 0.0 copy-done.4
  12.6 4.2 fusion.12
  16.8 12.2 %copy.19 = f32[1024,8,4,16]{3,2,1,0:T(4,128)} copy(f32[1024,8,4,16]{0,3,2,1:T(8,128)S(1)} %fusion.12) | data formatting | bytes 4194304 | tf_op jit(solution)/shard_map/abcd,de->abce/dot_general | solution.py:15
  29.0 15.5 %reshape.31 = f32[4,1,131072]{2,1,0:T(1,128)} reshape(f32[1024,8,4,16]{3,2,1,0:T(4,128)} %copy.19) | data formatting | bytes 4194304
  44.5 4.4 all-to-all-start
  48.9 26.7 %all_gather.6 = f32[32,32]{1,0:T(8,128)S(1)} all-gather(f32[8,32]{1,0:T(8,128)S(1)} %copy-done.5), channel_id=1, replica_groups=mesh['row'=4,'col'=8] {'row'}, dimensions={0}, use_global_device_ids=true | all-gather | bytes 5120 | tf_op jit(solution)/shard_map/all_gather | solution.py:16
  75.5 0.0 all-to-all-done
  75.5 1.4 copy-done.2
  76.9 0.5 broadcast.53
  77.4 7.7 %reduce.6 = f32[4,131072]{1,0:T(4,128)S(1)} reduce(f32[4,1,131072]{2,1,0:T(1,128)} %copy-done.2, f32[]{:T(128)} %broadcast.53), dimensions={1}, to_apply=%all_to_all.50.reduce_sub_computation | reduce | bytes 4194308 | tf_op jit(solution)/shard_map/all_to_all | solution.py:17
  85.1 17.9 %reshape.32 = f32[1024,8,4,16]{3,2,1,0:T(4,128)} reshape(f32[4,131072]{1,0:T(4,128)S(1)} %reduce.6) | data formatting | bytes 4194304
  103.0 12.2 %copy.20 = f32[4,256,8,4,16]{1,2,0,4,3:T(8,128)S(1)} copy(f32[4,256,8,4,16]{4,3,2,1,0:T(4,128)} %bitcast.72) | data formatting | bytes 4194304 | tf_op jit(solution)/shard_map/all_to_all | solution.py:17
  115.3 1.9 fusion.2
  117.2 1.2 copy.21
  118.4 28.1 %all_to_all.69 = f32[256,32,4,16]{0,3,2,1:T(8,128)S(1)} all-to-all(f32[256,32,4,16]{0,3,2,1:T(8,128)S(1)} %copy.21), channel_id=1, replica_groups=mesh['row'=4,'col'=8] {'row'}, dimensions={1} | all-to-all | bytes 4194304 | tf_op jit(solution)/shard_map/all_to_all | solution.py:19
  146.6 12.1 %copy.37 = f32[256,4,8,4,16]{4,3,2,0,1:T(4,128)} copy(f32[256,4,8,4,16]{0,4,3,2,1:T(8,128)S(1)} %bitcast.78) | data formatting | bytes 4194304 | tf_op jit(solution)/shard_map/all_to_all | solution.py:19
  158.6 15.4 %reshape.33 = f32[8,1,65536]{2,1,0:T(1,128)} reshape(f32[1024,8,4,16]{3,2,1,0:T(4,128)} %bitcast.73) | data formatting | bytes 4194304
  174.0 6.8 %all-to-all-start.2 = ((f32[8,1,65536]{2,1,0:T(1,128)}), f32[8,1,65536]{2,1,0:T(1,128)}, u32[]{:S(2)}, u32[]{:S(2)}) async-start(f32[8,1,65536]{2,1,0:T(1,128)} %reshape.33), calls=%async_computation.2 | async-start | bytes 4194304 | tf_op jit(solution)/shard_map/all_to_all | solution.py:21
  180.8 0.0 all-reduce.2.cloned.1.call-start
  180.9 66.5 %all-gather = f32[8,4,32]{2,1,0:T(4,128)S(1)} all-gather(f32[1,4,32]{2,1,0:T(4,128)S(1)} %bitcast.85), channel_id=1, replica_groups=mesh['row'=4,'col'=8] {'col'}, dimensions={0}, use_global_device_ids=true | all-gather | bytes 4608 | tf_op jit(solution)/shard_map/all_gather | solution.py:20
  247.3 0.0 all-to-all-done.2
  247.3 7.2 %reduce.7 = f32[8,65536]{1,0:T(8,128)S(1)} reduce(f32[8,1,65536]{2,1,0:T(1,128)} %all-to-all-done.2, f32[]{:T(128)} %broadcast.53), dimensions={1}, to_apply=%all_to_all.58.reduce_sub_computation | reduce | bytes 4194308 | tf_op jit(solution)/shard_map/all_to_all | solution.py:21
  254.6 17.3 %reshape.34 = f32[1024,8,4,16]{3,2,1,0:T(4,128)} reshape(f32[8,65536]{1,0:T(8,128)S(1)} %reduce.7) | data formatting | bytes 4194304
  271.9 9.8 %copy.35 = f32[8,128,8,4,16]{1,0,4,3,2:T(8,128)S(1)} copy(f32[8,128,8,4,16]{4,3,2,1,0:T(4,128)} %bitcast.74) | data formatting | bytes 4194304 | tf_op jit(solution)/shard_map/all_to_all | solution.py:21
  281.7 1.4 copy.25
  283.1 1.9 convolution_bitcast_fusion
  285.0 1.2 copy.27
  286.2 46.2 %all_to_all.70 = f32[128,8,32,16]{0,3,1,2:T(8,128)S(1)} all-to-all(f32[128,8,32,16]{0,3,1,2:T(8,128)S(1)} %copy.27), channel_id=1, replica_groups=mesh['row'=4,'col'=8] {'col'}, dimensions={2} | all-to-all | bytes 4194304 | tf_op jit(solution)/shard_map/all_to_all | solution.py:23
  332.5 1.2 copy.28
  333.7 8.9 %fusion.14 = f32[1024,1024]{1,0:T(8,128)} fusion(f32[64,8,8,128]{3,2,1,0:T(8,128)S(1)} %bitcast.75), kind=kOutput, calls=%fused_computation.20 | convolution fusion | flops 6442450944 | bytes 6291456 | tf_op jit(solution)/shard_map/dot_general | solution.py:26
  342.6 0.0 all-reduce.2.cloned.1.call-update
  342.7 1.9 copy.41
  344.5 138.8 %all-reduce.2.cloned.1.call-done = f32[1024,1024]{1,0:T(8,128)} async-done(((f32[1024,1024]{1,0:T(8,128)}), f32[1024,1024]{1,0:T(8,128)}) %all-reduce.2.cloned.1.call-update) | async-done | bytes 4194320 | tf_op jit(solution)/shard_map/psum | solution.py:27
  483.4 6.3 %fusion.15 = f32[1024,64]{0,1:T(8,128)S(1)} fusion(f32[1024,1024]{1,0:T(8,128)} %all-reduce.2.cloned.1.call-done, f32[1024,64]{0,1:T(8,128)S(1)} %copy-done), kind=kOutput, calls=%fused_computation.21 | convolution fusion | flops 805306368 | bytes 4718592 | tf_op jit(solution)/shard_map/dot_general | solution.py:28
  489.7 0.4 fusion.16
  490.1 0.1 copy.29
  490.2 5.8 %cholesky.16 = f32[64,64]{1,0:T(8,128)S(1)} custom-call(f32[64,64]{1,0:T(8,128)S(1)} %fusion.10), custom_call_target="Cholesky" | custom-call | tf_op jit(solution)/shard_map/jit(cholesky)/cholesky | solution.py:30
  496.0 0.6 compare_reduce_fusion
  496.7 0.7 fusion.7
  497.3 4.9 custom-call.7
  502.2 0.4 fusion.8
  502.7 0.0 copy-start.3
  502.7 0.0 copy-done.1
  502.7 2.5 fusion.5
  505.2 0.0 copy-done.3
  (9 shorter events, 0.1 us)
Async XLA Ops:
  7.2 476.2 %copy-start = (f32[1024,64]{0,1:T(8,128)S(1)}, f32[1024,64]{0,1:T(8,128)}, u32[]{:S(2)}) copy-start(f32[1024,64]{0,1:T(8,128)} %param.9) | copy-start | bytes 786436
  7.2 5.5 %copy-start.4 = (f32[32,16]{0,1:T(8,128)S(1)}, f32[32,16]{0,1:T(8,128)}, u32[]{:S(2)}) copy-start(f32[32,16]{0,1:T(8,128)} %param.8) | copy-start | bytes 6148
  44.5 4.4 copy-start.5
  44.5 31.1 %all-to-all-start = ((f32[4,1,131072]{2,1,0:T(1,128)}), f32[4,1,131072]{2,1,0:T(1,128)S(1)}, u32[]{:S(2)}, u32[]{:S(2)}) async-start(f32[4,1,131072]{2,1,0:T(1,128)} %reshape.31), calls=%async_computation | async-start | bytes 4194304 | tf_op jit(solution)/shard_map/all_to_all | solution.py:17
  75.5 1.4 copy-start.2
  174.0 6.8 %copy-start.6 = (f32[4,32]{1,0:T(4,128)S(1)}, f32[4,32]{1,0:T(4,128)}, u32[]{:S(2)}) copy-start(f32[4,32]{1,0:T(4,128)} %param.7) | copy-start | bytes 1540
  174.0 73.3 %all-to-all-start.2 = ((f32[8,1,65536]{2,1,0:T(1,128)}), f32[8,1,65536]{2,1,0:T(1,128)}, u32[]{:S(2)}, u32[]{:S(2)}) async-start(f32[8,1,65536]{2,1,0:T(1,128)} %reshape.33), calls=%async_computation.2 | async-start | bytes 4194304 | tf_op jit(solution)/shard_map/all_to_all | solution.py:21
  180.8 302.5 %all-reduce.2.cloned.1.call-start = ((), (), s32[]{:S(2)}) async-start(), calls=%async_computation.4 | async-start | bytes 8388608 | tf_op jit(solution)/shard_map/psum | solution.py:27
  344.5 158.2 %copy-start.1 = (f32[64,8,8,128]{3,1,2,0:T(8,128)S(1)}, f32[64,8,8,128]{3,1,2,0:T(8,128)}, u32[]{:S(2)}) copy-start(f32[64,8,8,128]{3,1,2,0:T(8,128)} %copy.41) | copy-start | bytes 6291460
  502.7 2.5 copy-start.3
Sparse Core Ops, SparseCore 0:
  342.8 140.5 all-reduce.1
where the time goes:
time: 518 us; the launch traced here: 512 us
  blocking collectives  168 us (32%)
  waiting for transfers between devices  139 us (27%)
  local copies, waits for them, and re-layouts  127 us (25%)
  other arithmetic  27 us (5%)
  matrix products  26.5 us (5%)
  between operations  14.6 us (3%)
  starting transfers between devices  11.2 us (2%)
    psum x1, waiting for transfers between devices, shards(): gram = lax.psum(local_gram, ('row', 'col'))  139 us
    unnamed x20, local copies, waits for them, and re-layouts  74.8 us
    all_gather x1, blocking collectives, shards(): whole_three = lax.all_gather(factor_three, 'col', axis=0, tiled=True)  66.5 us
    all_to_all x1, blocking collectives, shards(): lax.all_to_all(projected_three, 'col', split_axis=2, concat_axis=0, tiled...  46.2 us
    all_to_all x1, blocking collectives, shards(): lax.all_to_all(projected_two, 'row', split_axis=1, concat_axis=0, tiled=T...  28.1 us
    all_gather x1, blocking collectives, shards(): whole_two = lax.all_gather(factor_two, 'row', axis=0, tiled=True)  26.7 us
    all_to_all x2, local copies, waits for them, and re-layouts, shards(): lax.all_to_all(fourth, 'row', split_axis=0, concat_axis=1, tiled=True)  12.7 us
    dot_general x1, local copies, waits for them, and re-layouts, shards(): fourth = jnp.einsum('abcd,de->abce', data, factor_four, precision=highest)  12.2 us
  transfers between devices with their start and end apart: 3, of which 1 were waited for; matrix products, arithmetic and copies ran while one was open for 0% of the time, Pallas kernels for 0%

commit v1 on v0

--- a/solution.py
+++ b/solution.py
@@ -24,7 +24,7 @@
     columns = block.reshape(first_len, -1)
     basis = factor_init
     local_gram = jnp.dot(columns, columns.T, precision=highest, preferred_element_type=jnp.float32)
-    gram = lax.psum(local_gram, ("row", "col"))
+    gram = lax.psum(lax.psum(local_gram, "col"), axis_name="row")
     image = jnp.dot(gram, basis, precision=highest, preferred_element_type=jnp.float32)
     square = jnp.dot(image.T, image, precision=highest, preferred_element_type=jnp.float32)
     lower = jnp.linalg.cholesky(square)

time: 518 us -> 619 us (1.19)
  waiting for transfers between devices: 139 us -> 240 us
    psum x1 -> x2, waiting for transfers between devices: 139 us -> 239 us  [shards(): gram = lax.psum(lax.psum(local_gram, 'col'), axis_name='row')]
  transfers between devices with their start and end apart: 3 -> 4, of which waited for: 1 -> 2; matrix products, arithmetic and copies ran while one was open for 0% -> 0% of each run, Pallas kernels for 0% -> 0%
where the time goes in v1:
time: 619 us; the launch traced here: 613 us
  waiting for transfers between devices  240 us (39%)
  blocking collectives  168 us (27%)
  local copies, waits for them, and re-layouts  127 us (21%)
  other arithmetic  27 us (4%)
  matrix products  26.3 us (4%)
  between operations  14.6 us (2%)
  starting transfers between devices  11.5 us (2%)
    psum x2, waiting for transfers between devices, shards(): gram = lax.psum(lax.psum(local_gram, 'col'), axis_name='row')  239 us
    unnamed x20, local copies, waits for them, and re-layouts  74.8 us
    all_gather x1, blocking collectives, shards(): whole_three = lax.all_gather(factor_three, 'col', axis=0, tiled=True)  66.5 us
    all_to_all x1, blocking collectives, shards(): lax.all_to_all(projected_three, 'col', split_axis=2, concat_axis=0, tiled...  46.2 us
    all_to_all x1, blocking collectives, shards(): lax.all_to_all(projected_two, 'row', split_axis=1, concat_axis=0, tiled=T...  28.1 us
    all_gather x1, blocking collectives, shards(): whole_two = lax.all_gather(factor_two, 'row', axis=0, tiled=True)  26.7 us
    all_to_all x2, local copies, waits for them, and re-layouts, shards(): lax.all_to_all(fourth, 'row', split_axis=0, concat_axis=1, tiled=True)  12.7 us
  transfers between devices with their start and end apart: 4, of which 2 were waited for; matrix products, arithmetic and copies ran while one was open for 0% of the time, Pallas kernels for 0%

profile of v1, /device:TPU:0, one launch (start us, length us, event | category | flops | bytes accessed | tf_op | source)
XLA Modules:
  0.0 613.2 jit_solution(8120457811171776811)
XLA Ops:
  7.2 0.0 copy-start
  7.2 5.5 copy.18
  12.6 0.0 copy-done.4
  12.6 4.2 fusion.12
  16.8 12.2 %copy.19 = f32[1024,8,4,16]{3,2,1,0:T(4,128)} copy(f32[1024,8,4,16]{0,3,2,1:T(8,128)S(1)} %fusion.12) | data formatting | bytes 4194304 | tf_op jit(solution)/shard_map/abcd,de->abce/dot_general | solution.py:15
  29.0 15.5 %reshape.31 = f32[4,1,131072]{2,1,0:T(1,128)} reshape(f32[1024,8,4,16]{3,2,1,0:T(4,128)} %copy.19) | data formatting | bytes 4194304
  44.5 4.4 all-to-all-start
  48.9 26.7 %all_gather.6 = f32[32,32]{1,0:T(8,128)S(1)} all-gather(f32[8,32]{1,0:T(8,128)S(1)} %copy-done.5), channel_id=1, replica_groups=mesh['row'=4,'col'=8] {'row'}, dimensions={0}, use_global_device_ids=true | all-gather | bytes 5120 | tf_op jit(solution)/shard_map/all_gather | solution.py:16
  75.5 0.0 all-to-all-done
  75.5 1.4 copy-done.2
  76.9 0.5 broadcast.53
  77.4 7.7 %reduce.6 = f32[4,131072]{1,0:T(4,128)S(1)} reduce(f32[4,1,131072]{2,1,0:T(1,128)} %copy-done.2, f32[]{:T(128)} %broadcast.53), dimensions={1}, to_apply=%all_to_all.50.reduce_sub_computation | reduce | bytes 4194308 | tf_op jit(solution)/shard_map/all_to_all | solution.py:17
  85.1 17.9 %reshape.32 = f32[1024,8,4,16]{3,2,1,0:T(4,128)} reshape(f32[4,131072]{1,0:T(4,128)S(1)} %reduce.6) | data formatting | bytes 4194304
  103.0 12.2 %copy.20 = f32[4,256,8,4,16]{1,2,0,4,3:T(8,128)S(1)} copy(f32[4,256,8,4,16]{4,3,2,1,0:T(4,128)} %bitcast.72) | data formatting | bytes 4194304 | tf_op jit(solution)/shard_map/all_to_all | solution.py:17
  115.3 1.9 fusion.2
  117.2 1.2 copy.21
  118.4 28.1 %all_to_all.69 = f32[256,32,4,16]{0,3,2,1:T(8,128)S(1)} all-to-all(f32[256,32,4,16]{0,3,2,1:T(8,128)S(1)} %copy.21), channel_id=1, replica_groups=mesh['row'=4,'col'=8] {'row'}, dimensions={1} | all-to-all | bytes 4194304 | tf_op jit(solution)/shard_map/all_to_all | solution.py:19
  146.6 12.1 %copy.37 = f32[256,4,8,4,16]{4,3,2,0,1:T(4,128)} copy(f32[256,4,8,4,16]{0,4,3,2,1:T(8,128)S(1)} %bitcast.78) | data formatting | bytes 4194304 | tf_op jit(solution)/shard_map/all_to_all | solution.py:19
  158.6 15.4 %reshape.33 = f32[8,1,65536]{2,1,0:T(1,128)} reshape(f32[1024,8,4,16]{3,2,1,0:T(4,128)} %bitcast.73) | data formatting | bytes 4194304
  174.0 6.8 %all-to-all-start.2 = ((f32[8,1,65536]{2,1,0:T(1,128)}), f32[8,1,65536]{2,1,0:T(1,128)}, u32[]{:S(2)}, u32[]{:S(2)}) async-start(f32[8,1,65536]{2,1,0:T(1,128)} %reshape.33), calls=%async_computation.2 | async-start | bytes 4194304 | tf_op jit(solution)/shard_map/all_to_all | solution.py:21
  180.8 0.0 all-reduce.3.cloned.1.call-start
  180.9 66.5 %all-gather = f32[8,4,32]{2,1,0:T(4,128)S(1)} all-gather(f32[1,4,32]{2,1,0:T(4,128)S(1)} %bitcast.85), channel_id=1, replica_groups=mesh['row'=4,'col'=8] {'col'}, dimensions={0}, use_global_device_ids=true | all-gather | bytes 4608 | tf_op jit(solution)/shard_map/all_gather | solution.py:20
  247.3 0.0 all-to-all-done.2
  247.3 7.2 %reduce.7 = f32[8,65536]{1,0:T(8,128)S(1)} reduce(f32[8,1,65536]{2,1,0:T(1,128)} %all-to-all-done.2, f32[]{:T(128)} %broadcast.53), dimensions={1}, to_apply=%all_to_all.58.reduce_sub_computation | reduce | bytes 4194308 | tf_op jit(solution)/shard_map/all_to_all | solution.py:21
  254.6 17.3 %reshape.34 = f32[1024,8,4,16]{3,2,1,0:T(4,128)} reshape(f32[8,65536]{1,0:T(8,128)S(1)} %reduce.7) | data formatting | bytes 4194304
  271.9 9.8 %copy.35 = f32[8,128,8,4,16]{1,0,4,3,2:T(8,128)S(1)} copy(f32[8,128,8,4,16]{4,3,2,1,0:T(4,128)} %bitcast.74) | data formatting | bytes 4194304 | tf_op jit(solution)/shard_map/all_to_all | solution.py:21
  281.7 1.4 copy.25
  283.1 1.9 convolution_bitcast_fusion
  285.0 1.2 copy.27
  286.2 46.2 %all_to_all.70 = f32[128,8,32,16]{0,3,1,2:T(8,128)S(1)} all-to-all(f32[128,8,32,16]{0,3,1,2:T(8,128)S(1)} %copy.27), channel_id=1, replica_groups=mesh['row'=4,'col'=8] {'col'}, dimensions={2} | all-to-all | bytes 4194304 | tf_op jit(solution)/shard_map/all_to_all | solution.py:23
  332.5 1.2 copy.28
  333.7 8.7 %fusion.14 = f32[1024,1024]{1,0:T(8,128)} fusion(f32[64,8,8,128]{3,2,1,0:T(8,128)S(1)} %bitcast.75), kind=kOutput, calls=%fused_computation.20 | convolution fusion | flops 6442450944 | bytes 6291456 | tf_op jit(solution)/shard_map/dot_general | solution.py:26
  342.4 0.0 all-reduce.3.cloned.1.call-update
  342.4 0.3 all-reduce.5.cloned.1.call-start
  342.7 154.5 %all-reduce.3.cloned.1.call-done = f32[1024,1024]{1,0:T(8,128)} async-done(((f32[1024,1024]{1,0:T(8,128)}), f32[1024,1024]{1,0:T(8,128)}) %all-reduce.3.cloned.1.call-update) | async-done | bytes 4194320 | tf_op jit(solution)/shard_map/psum | solution.py:27
  497.2 0.0 all-reduce.5.cloned.1.call-update
  497.3 1.9 copy.41
  499.1 85.0 %all-reduce.5.cloned.1.call-done = f32[1024,1024]{1,0:T(8,128)} async-done(((f32[1024,1024]{1,0:T(8,128)}), f32[1024,1024]{1,0:T(8,128)}) %all-reduce.5.cloned.1.call-update) | async-done | bytes 4194320 | tf_op jit(solution)/shard_map/psum | solution.py:27
  584.1 6.3 %fusion.15 = f32[1024,64]{0,1:T(8,128)S(1)} fusion(f32[1024,1024]{1,0:T(8,128)} %all-reduce.5.cloned.1.call-done, f32[1024,64]{0,1:T(8,128)S(1)} %copy-done), kind=kOutput, calls=%fused_computation.21 | convolution fusion | flops 805306368 | bytes 4718592 | tf_op jit(solution)/shard_map/dot_general | solution.py:28
  590.4 0.4 fusion.16
  590.8 0.1 copy.29
  590.9 5.8 cholesky.16
  596.8 0.6 compare_reduce_fusion
  597.4 0.7 fusion.7
  598.1 4.9 custom-call.7
  603.0 0.4 fusion.8
  603.4 0.0 copy-start.3
  603.4 2.5 fusion.5
  (12 shorter events, 0.1 us)
Async XLA Ops:
  7.2 576.9 %copy-start = (f32[1024,64]{0,1:T(8,128)S(1)}, f32[1024,64]{0,1:T(8,128)}, u32[]{:S(2)}) copy-start(f32[1024,64]{0,1:T(8,128)} %param.9) | copy-start | bytes 786436
  7.2 5.5 copy-start.4
  44.5 4.4 copy-start.5
  44.5 31.1 %all-to-all-start = ((f32[4,1,131072]{2,1,0:T(1,128)}), f32[4,1,131072]{2,1,0:T(1,128)S(1)}, u32[]{:S(2)}, u32[]{:S(2)}) async-start(f32[4,1,131072]{2,1,0:T(1,128)} %reshape.31), calls=%async_computation | async-start | bytes 4194304 | tf_op jit(solution)/shard_map/all_to_all | solution.py:17
  75.5 1.4 copy-start.2
  174.0 6.8 %copy-start.6 = (f32[4,32]{1,0:T(4,128)S(1)}, f32[4,32]{1,0:T(4,128)}, u32[]{:S(2)}) copy-start(f32[4,32]{1,0:T(4,128)} %param.7) | copy-start | bytes 1540
  174.0 73.3 %all-to-all-start.2 = ((f32[8,1,65536]{2,1,0:T(1,128)}), f32[8,1,65536]{2,1,0:T(1,128)}, u32[]{:S(2)}, u32[]{:S(2)}) async-start(f32[8,1,65536]{2,1,0:T(1,128)} %reshape.33), calls=%async_computation.2 | async-start | bytes 4194304 | tf_op jit(solution)/shard_map/all_to_all | solution.py:21
  180.8 316.4 %all-reduce.3.cloned.1.call-start = ((), (), s32[]{:S(2)}) async-start(), calls=%async_computation.4 | async-start | bytes 8388608 | tf_op jit(solution)/shard_map/psum | solution.py:27
  342.4 241.7 %all-reduce.5.cloned.1.call-start = ((), (), s32[]{:S(2)}) async-start(), calls=%async_computation.5 | async-start | bytes 8388608 | tf_op jit(solution)/shard_map/psum | solution.py:27
  499.1 104.3 %copy-start.1 = (f32[64,8,8,128]{3,1,2,0:T(8,128)S(1)}, f32[64,8,8,128]{3,1,2,0:T(8,128)}, u32[]{:S(2)}) copy-start(f32[64,8,8,128]{3,1,2,0:T(8,128)} %copy.41) | copy-start | bytes 6291460
  603.4 2.5 copy-start.3
Sparse Core Ops, SparseCore 0:
  342.6 154.6 all-reduce.2
  499.6 84.4 all-reduce.4
